TPU v7x, 128 devices: a whole 4x4x4 slice. The times are simulated.
128 devices in a mesh: zero: 16 (over z, y), width: 8 (over x, core).
Axes of the slice: x: 4, y: 4, z: 4, core: 2. Of those that a mesh axis runs over, the one named last changes fastest.
Arguments:
- train_query: float32 [7168, 7168], P('zero', 'width'), may hold values from -0.09375 to 0.09375
- slow_query: float32 [7168, 7168], P('zero', 'width'), may hold values from -0.0625 to 0.0625
- train_key: float32 [7168, 1024], P('zero', 'width'), may hold values from -0.09375 to 0.09375
- slow_key: float32 [7168, 1024], P('zero', 'width'), may hold values from -0.0625 to 0.0625
- train_value: float32 [7168, 1024], P('zero', 'width'), may hold values from -0.09375 to 0.09375
- slow_value: float32 [7168, 1024], P('zero', 'width'), may hold values from -0.0625 to 0.0625
- norm_train: float32 [7168], P(('zero', 'width')), may hold values from 0.25 to 1.75
- norm_step: float32 [7168], P(('zero', 'width')), may hold values from -0.3 to 0.3
Outputs:
- ready_query: bfloat16 [7168, 7168], P(None, 'width')
- ready_key: bfloat16 [7168, 1024], P(None, 'width')
- ready_value: bfloat16 [7168, 1024], P(None, 'width')
- scale_query: float32 [7168], P('width')
- scale_key: float32 [1024], P('width')
- scale_value: float32 [1024], P('width')
- serve_norm: bfloat16 [7168], replicated
- latest_query: float32 [7168, 7168], P('zero', 'width')
- latest_key: float32 [7168, 1024], P('zero', 'width')
- latest_value: float32 [7168, 1024], P('zero', 'width')
All inputs are finite; a program needn't handle non-finite values.
Results may differ from a plain program's by a relative error of at most 0.0004.
Values may be sent and summed in bfloat16 or wider, within the bound.
A program may use at most 128 MiB of HBM per device.

v0:
```python
import jax
import jax.numpy as jnp
from jax import lax
from jax.sharding import PartitionSpec as P

keep_rate = 0.5


def sent_to_all(array, axis):
    size = lax.axis_size(axis)
    return lax.all_to_all(
        jnp.broadcast_to(array[None], (size, *array.shape)), axis, 0, 0, tiled=True
    )


def over_copies(array, axis):
    everything = sent_to_all(array, axis)
    return jnp.sum(everything, axis=0)


def together(arrays, axis):
    line, at, outs = (jnp.concatenate([a.reshape(-1) for a in arrays]), 0, [])
    running = over_copies(line, axis)
    for a in arrays:
        outs.append(running[at : at + a.size].reshape(a.shape))
        at += a.size
    return tuple(outs)


def sent_together(arrays, axis, dim, along):
    widths = [a.shape[along] for a in arrays]
    both = jnp.concatenate(arrays, axis=along)
    whole = lax.all_gather(both, axis, axis=dim, tiled=True)
    return tuple(jnp.split(whole, [sum(widths[:k]) for k in range(1, len(widths))], axis=along))


def body(
    train_query, slow_query, train_key, slow_key, train_value, slow_value, norm_train, norm_step
):
    latest_query = keep_rate * slow_query + (1.0 - keep_rate) * train_query
    latest_key = keep_rate * slow_key + (1.0 - keep_rate) * train_key
    latest_value = keep_rate * slow_value + (1.0 - keep_rate) * train_value
    total_query, total_key, total_value = together(
        (
            jnp.sum(latest_query * latest_query, axis=0),
            jnp.sum(latest_key * latest_key, axis=0),
            jnp.sum(latest_value * latest_value, axis=0),
        ),
        "zero",
    )
    scale_query = jnp.sqrt(total_query)
    scale_key = jnp.sqrt(total_key)
    scale_value = jnp.sqrt(total_value)
    narrow_query, narrow_key, narrow_value = (
        (latest_query / scale_query).astype(jnp.bfloat16),
        (latest_key / scale_key).astype(jnp.bfloat16),
        (latest_value / scale_value).astype(jnp.bfloat16),
    )
    ready_query, ready_key, ready_value = sent_together(
        (narrow_query, narrow_key, narrow_value), "zero", 0, 1
    )
    serve_norm = lax.all_gather(
        (norm_train + norm_step).astype(jnp.bfloat16), ("zero", "width"), axis=0, tiled=True
    )
    return (
        ready_query,
        ready_key,
        ready_value,
        scale_query,
        scale_key,
        scale_value,
        serve_norm,
        latest_query,
        latest_key,
        latest_value,
    )


def solution(mesh):
    in_specs = (
        P("zero", "width"),
        P("zero", "width"),
        P("zero", "width"),
        P("zero", "width"),
        P("zero", "width"),
        P("zero", "width"),
        P(("zero", "width")),
        P(("zero", "width")),
    )
    out_specs = (
        P(None, "width"),
        P(None, "width"),
        P(None, "width"),
        P("width"),
        P("width"),
        P("width"),
        P(),
        P("zero", "width"),
        P("zero", "width"),
        P("zero", "width"),
    )
    return jax.shard_map(body, mesh=mesh, in_specs=in_specs, out_specs=out_specs, check_vma=False)
```

profile of v0, /device:TPU:0, one launch (start us, length us, event | category | flops | bytes accessed | tf_op | source)
XLA Modules:
  0.0 157.4 jit_solution(17647005165624234533)
XLA Ops:
  7.2 0.0 copy-start.6
  7.2 0.0 copy-start.5
  7.2 0.0 copy-start.4
  7.2 0.0 copy-start.3
  7.2 0.0 all-gather.2.cloned.1.call-start
  7.3 2.3 %multiply_reduce_fusion = (f32[896]{0:T(1024)S(1)}, f32[448,896]{1,0:T(8,128)S(1)}) fusion(f32[448,896]{1,0:T(8,128)} %param.9, f32[448,896]{1,0:T(8,128)} %param.8), kind=kLoop, calls=%fused_computation.1 | loop fusion | flops 1604736 | bytes 4820480 | tf_op jit(solution)/shard_map/reduce_sum | solution.py:45
  9.5 0.0 copy-done.6
  9.5 0.0 copy-done.5
  9.6 0.0 copy-done.4
  9.6 0.0 copy-done.3
  9.6 0.0 copy-start
  9.6 0.1 multiply_reduce_fusion.1
  9.7 0.0 copy-start.1
  9.7 0.0 copy-start.2
  9.8 15.6 %all_to_all.6 = f32[16,1,1152]{2,1,0:T(1,128)S(1)} all-to-all(f32[16,1,1152]{2,1,0:T(1,128)S(1)} %broadcast_in_dim.2), channel_id=1, replica_groups=mesh['zero'=16,'width'=8] {'zero'}, dimensions={0} | all-to-all | bytes 147456 | tf_op jit(solution)/shard_map/all_to_all | solution.py:11
  25.4 0.1 reduce_sum.39
  25.5 0.0 copy-start.8
  25.5 0.0 copy-start.9
  25.5 0.0 copy-start.7
  25.6 0.1 divide_convert_fusion
  25.7 0.0 copy-done
  25.7 0.0 copy-start.10
  25.7 0.0 copy-start.11
  25.7 1.1 pad_maximum_fusion
  26.8 0.0 copy-done.9
  26.8 0.0 copy-done.7
  26.8 0.0 all-gather.2.cloned.1.call-update
  26.9 0.2 dynamic-update-slice
  27.1 66.3 %all-reduce = bf16[7168]{0:T(1024)(128)(2,1)} all-reduce(bf16[7168]{0:T(1024)(128)(2,1)S(1)} %dynamic-update-slice), channel_id=1, replica_groups=mesh['zero'=16,'width'=8] {'zero','width'}, use_global_device_ids=true, to_apply=%add | all-reduce | flops 7168 | bytes 28672
  93.5 42.3 %all-gather.2.cloned.1.call-done = bf16[7168,1152]{1,0:T(8,128)(2,1)} async-done(((bf16[448,1152]{1,0:T(8,128)(2,1)}), bf16[7168,1152]{1,0:T(8,128)(2,1)}) %all-gather.2.cloned.1.call-update) | async-done | bytes 16515088 | tf_op jit(solution)/shard_map/all_gather | solution.py:33
  135.8 4.1 %fusion = (bf16[7168,128]{1,0:T(8,128)(2,1)}, bf16[7168,128]{1,0:T(8,128)(2,1)}) fusion(bf16[7168,1152]{1,0:T(8,128)(2,1)} %all-gather.2.cloned.1.call-done), kind=kLoop, calls=%fused_computation.15 | loop fusion | bytes 7340032 | tf_op jit(solution)/shard_map/split | solution.py:34
  139.9 10.7 %split.12 = bf16[7168,896]{1,0:T(8,128)(2,1)} slice(bf16[7168,1152]{1,0:T(8,128)(2,1)} %all-gather.2.cloned.1.call-done), slice={[0:7168], [0:896]} | slice | bytes 25690112 | tf_op jit(solution)/shard_map/split | solution.py:34
  (13 shorter events, 0.1 us)
Async XLA Ops:
  7.2 2.4 %copy-start.6 = (f32[448,128]{1,0:T(8,128)S(1)}, f32[448,128]{1,0:T(8,128)}, u32[]{:S(2)}) copy-start(f32[448,128]{1,0:T(8,128)} %param.10) | copy-start | bytes 688132
  7.2 2.4 %copy-start.5 = (f32[448,128]{1,0:T(8,128)S(1)}, f32[448,128]{1,0:T(8,128)}, u32[]{:S(2)}) copy-start(f32[448,128]{1,0:T(8,128)} %param.11) | copy-start | bytes 688132
  7.2 2.4 %copy-start.4 = (f32[448,128]{1,0:T(8,128)S(1)}, f32[448,128]{1,0:T(8,128)}, u32[]{:S(2)}) copy-start(f32[448,128]{1,0:T(8,128)} %param.12) | copy-start | bytes 688132
  7.2 2.4 %copy-start.3 = (f32[448,128]{1,0:T(8,128)S(1)}, f32[448,128]{1,0:T(8,128)}, u32[]{:S(2)}) copy-start(f32[448,128]{1,0:T(8,128)} %param.13) | copy-start | bytes 688132
  7.2 128.6 %all-gather.2.cloned.1.call-start = ((), (), s32[]{:S(2)}) async-start(), calls=%async_computation.1 | async-start | bytes 17547264 | tf_op jit(solution)/shard_map/all_gather | solution.py:33
  9.6 16.1 %copy-start = (f32[448,896]{1,0:T(8,128)}, f32[448,896]{1,0:T(8,128)S(1)}, u32[]{:S(2)}) copy-start(f32[448,896]{1,0:T(8,128)S(1)} %get-tuple-element.11) | copy-start | bytes 4816900
  9.7 17.1 %copy-start.1 = (f32[448,128]{1,0:T(8,128)}, f32[448,128]{1,0:T(8,128)S(1)}, u32[]{:S(2)}) copy-start(f32[448,128]{1,0:T(8,128)S(1)} %get-tuple-element.15) | copy-start | bytes 688132
  9.7 17.1 %copy-start.2 = (f32[448,128]{1,0:T(8,128)}, f32[448,128]{1,0:T(8,128)S(1)}, u32[]{:S(2)}) copy-start(f32[448,128]{1,0:T(8,128)S(1)} %get-tuple-element.21) | copy-start | bytes 688132
  25.5 1.3 copy-start.8
  25.5 1.3 copy-start.9
  25.5 1.3 copy-start.7
  25.7 1.1 copy-start.10
  25.7 1.1 copy-start.11
Sparse Core Ops, SparseCore 0:
  27.0 108.7 all-gather.1
where the time goes:
time: 158 us; the launch traced here: 157 us
  blocking collectives  82 us (52%)
  waiting for transfers between devices  42.3 us (27%)
  local copies, waits for them, and re-layouts  15.2 us (10%)
  between operations  14.3 us (9%)
  other arithmetic  3.64 us (2%)
    unnamed x1, blocking collectives  66.3 us
    all_gather x1, waiting for transfers between devices, sent_together(): whole = lax.all_gather(both, axis, axis=dim, tiled=True)  42.3 us
    all_to_all x1, blocking collectives, sent_to_all(): lax.all_to_all(jnp.broadcast_to(array[None], (size, *array.shape)), axis,...  15.6 us
    split x2, local copies, waits for them, and re-layouts, sent_together(): jnp.split(whole, [sum(widths[:k]) for k in range(1, len(widths))], axis=a...  14.8 us
  transfers between devices with their start and end apart: 1, of which 1 were waited for; matrix products, arithmetic and copies ran while one was open for 0% of the time, Pallas kernels for 0%

commit v1 on v0

v1 whole, which is shorter than its diff:
```python
import functools

import jax
import jax.numpy as jnp
from jax import lax
from jax.experimental import pallas as pl
from jax.experimental.pallas import tpu as pltpu
from jax.sharding import PartitionSpec as P

keep_rate = 0.5
MESH = pl.DeviceIdType.MESH

NZ, NY, NW = 4, 4, 8
NZERO = NZ * NY
ROWS = 448
WQ, WK = 896, 128
COLS = WQ + 2 * WK
QUARTER = ROWS // 4
SLAB = 16
NORM = 56

ORDER = (
    ("one", 0),
    ("two", 0, 0),
    ("one", 1),
    ("two", 1, 0),
    ("one", 2),
    ("two", 2, 0),
    ("two", 0, 1),
    ("two", 3, 0),
    ("two", 1, 1),
    ("two", 2, 1),
    ("two", 0, 2),
    ("two", 3, 1),
    ("two", 1, 2),
    ("two", 2, 2),
    ("two", 3, 2),
)
SLOT = {entry: at for at, entry in enumerate(ORDER)}
LINKS = (("y", 1), ("y", -1), ("z", 1), ("z", -1))
PARTNER = (2, 3, 0, 1)


def gather_kernel(
    tq, sq, tk, sk, tv, sv, nt, ns,
    all_ref, lat_ref, cq_ref, ck_ref, cv_ref, norm_ref,
    tbuf, sbuf, sums, ntb, nsb, nbuf,
    load_sem, nload_sem, sum_send, sum_recv, na_send, na_recv, nb_send, nb_recv,
    send_sem, recv_sem,
):
    me = lax.axis_index("zero")
    wide = lax.axis_index("width")
    z, y = me // NY, me % NY

    def at(zz, yy):
        return lax.rem(zz + 2 * NZ, NZ) * NY + lax.rem(yy + 2 * NY, NY)

    barrier = pltpu.get_barrier_semaphore()
    for d in range(1, NZERO):
        pl.semaphore_signal(
            barrier, inc=1, device_id=(lax.rem(me + d, NZERO), wide), device_id_type=MESH
        )
    for d in range(1, NW):
        pl.semaphore_signal(
            barrier, inc=1, device_id=(me, lax.rem(wide + d, NW)), device_id_type=MESH
        )

    loads = []
    for c in range(4):
        rows = pl.ds(c * QUARTER, QUARTER)
        group = []
        for i, (src, buf, first, width) in enumerate((
            (tq, tbuf, 0, WQ), (sq, sbuf, 0, WQ),
            (tk, tbuf, WQ, WK), (sk, sbuf, WQ, WK),
            (tv, tbuf, WQ + WK, WK), (sv, sbuf, WQ + WK, WK),
        )):
            copy = pltpu.make_async_copy(
                src.at[rows], buf.at[rows, pl.ds(first, width)], load_sem.at[c, i]
            )
            copy.start()
            group.append(copy)
        loads.append(group)
    nload = (
        pltpu.make_async_copy(nt, ntb, nload_sem.at[0]),
        pltpu.make_async_copy(ns, nsb, nload_sem.at[1]),
    )
    for copy in nload:
        copy.start()

    acc = jnp.zeros((8, COLS), jnp.float32)
    for c in range(4):
        for copy in loads[c]:
            copy.wait()

        def average(i, acc):
            rows = pl.ds(pl.multiple_of(c * QUARTER + i * SLAB, SLAB), SLAB)
            latest = keep_rate * sbuf[rows, :] + (1.0 - keep_rate) * tbuf[rows, :]
            lat_ref[rows, :] = latest
            square = latest * latest
            return acc + square[:8] + square[8:]

        acc = lax.fori_loop(0, QUARTER // SLAB, average, acc)
    sums[me] = jnp.sum(acc, axis=0, keepdims=True)
    for copy in nload:
        copy.wait()
    mine = (ntb[...] + nsb[...]).reshape(1, NORM)
    nbuf[me, wide] = jnp.concatenate([mine, jnp.zeros((1, 128 - NORM), jnp.float32)], axis=1)

    pl.semaphore_wait(barrier, NZERO - 1 + NW - 1)

    small = []
    for d in range(1, NZERO):
        copy = pltpu.make_async_remote_copy(
            src_ref=sums.at[me], dst_ref=sums.at[me],
            send_sem=sum_send.at[d], recv_sem=sum_recv.at[d],
            device_id=(lax.rem(me + d, NZERO), wide), device_id_type=MESH,
        )
        copy.start()
        small.append(copy)
    across = []
    for d in range(1, NW):
        copy = pltpu.make_async_remote_copy(
            src_ref=nbuf.at[me, wide], dst_ref=nbuf.at[me, wide],
            send_sem=na_send.at[d], recv_sem=na_recv.at[d],
            device_id=(me, lax.rem(wide + d, NW)), device_id_type=MESH,
        )
        copy.start()
        across.append(copy)
    for copy in small:
        copy.wait()

    total = sums[0]
    for d in range(1, NZERO):
        total = total + sums[d]
    scale = jnp.sqrt(total)
    for r in range(WQ // 128):
        cq_ref[pl.ds(r, 1), :] = scale[:, r * 128 : (r + 1) * 128]
    ck_ref[...] = scale[:, WQ : WQ + WK]
    cv_ref[...] = scale[:, WQ + WK :]
    inverse = jnp.broadcast_to(1.0 / scale, (SLAB, COLS))

    copies = {}

    def piece(p, zz, yy):
        first = at(zz, yy) * ROWS + p * QUARTER
        return pl.ds(pl.multiple_of(first, QUARTER), QUARTER)

    def start(link, slot):
        ring, sign = LINKS[link]
        entry = ORDER[slot]
        if entry[0] == "one":
            p, j, k = link, 0, entry[1]
            if k > 0:
                copies[link, SLOT["one", k - 1]].wait_recv()
            steps = {ring: k}
        else:
            p, j, k = PARTNER[link], entry[1], entry[2]
            if k > 0:
                copies[link, SLOT["two", j, k - 1]].wait_recv()
            elif j == 3:
                copies[p, SLOT["one", 2]].wait_recv()
            steps = {ring: k, LINKS[p][0]: j}
        rows = piece(p, z - sign * steps.get("z", 0), y - sign * steps.get("y", 0))
        target = at(z + sign, y) if ring == "z" else at(z, y + sign)
        copy = pltpu.make_async_remote_copy(
            src_ref=all_ref.at[rows], dst_ref=all_ref.at[rows],
            send_sem=send_sem.at[link, slot], recv_sem=recv_sem.at[link, slot],
            device_id=(target, wide), device_id_type=MESH,
        )
        copy.start()
        copies[link, slot] = copy

    for p in range(4):
        def narrow(i, _):
            rows = pl.ds(pl.multiple_of(p * QUARTER + i * SLAB, SLAB), SLAB)
            there = pl.ds(pl.multiple_of(me * ROWS + p * QUARTER + i * SLAB, SLAB), SLAB)
            all_ref[there, :] = (lat_ref[rows, :] * inverse).astype(jnp.bfloat16)
            return 0

        lax.fori_loop(0, QUARTER // SLAB, narrow, 0)
        start(p, 0)
    for link in range(4):
        start(link, 1)

    for copy in across:
        copy.wait()
    on = []
    for d in range(1, NZERO):
        copy = pltpu.make_async_remote_copy(
            src_ref=nbuf.at[me], dst_ref=nbuf.at[me],
            send_sem=nb_send.at[d], recv_sem=nb_recv.at[d],
            device_id=(lax.rem(me + d, NZERO), wide), device_id_type=MESH,
        )
        copy.start()
        on.append(copy)

    for slot in range(2, 6):
        for link in range(4):
            start(link, slot)

    for copy in on:
        copy.wait()
    lane = lax.broadcasted_iota(jnp.int32, (1, 128), 1)
    for r in range(NZERO * NW * NORM // 128):
        row = jnp.zeros((1, 128), jnp.float32)
        for d in range(128 * r // NORM, (128 * r + 127) // NORM + 1):
            shift = d * NORM - 128 * r
            moved = pltpu.roll(nbuf[d // NW, d % NW], shift % 128, 1)
            row = jnp.where((lane >= shift) & (lane < shift + NORM), moved, row)
        norm_ref[pl.ds(r, 1), :] = row

    for slot in range(6, len(ORDER)):
        for link in range(4):
            start(link, slot)

    for slot in range(len(ORDER)):
        for link in range(4):
            copies[link, slot].wait_send()
    waited = {("one", 0), ("one", 1), ("one", 2)}
    waited |= {("two", j, k) for j in range(4) for k in range(2)}
    for entry in ORDER:
        if entry not in waited:
            for link in range(4):
                copies[link, SLOT[entry]].wait_recv()


def write_kernel(
    all_ref, lat_ref, sq_ref, sk_ref, sv_ref, norm_ref,
    rq, rk, rv, cq, ck, cv, norm_out, lq, lk, lv,
    norm_buf, sem,
):
    copies = []
    for src, outs in ((all_ref, (rq, rk, rv)), (lat_ref, (lq, lk, lv))):
        first = 0
        for out in outs:
            width = out.shape[1]
            copies.append((src.at[:, pl.ds(first, width)], out))
            first += width
    copies += [(sq_ref, cq), (sk_ref, ck), (sv_ref, cv)]
    started = []
    for i, (src, dst) in enumerate(copies):
        copy = pltpu.make_async_copy(src, dst, sem.at[i])
        copy.start()
        started.append(copy)
    norm_buf[...] = norm_ref[...].astype(jnp.bfloat16)
    copy = pltpu.make_async_copy(norm_buf, norm_out, sem.at[len(copies)])
    copy.start()
    for done in started:
        done.wait()
    copy.wait()


def body(tq, sq, tk, sk, tv, sv, nt, ns):
    f32, bf16 = jnp.float32, jnp.bfloat16
    anyspace = pl.BlockSpec(memory_space=pl.ANY)
    hbm = pl.BlockSpec(memory_space=pltpu.HBM)
    dma = pltpu.SemaphoreType.DMA
    norm_rows = NZERO * NW * NORM // 128
    gathered = pl.pallas_call(
        gather_kernel,
        name="gather",
        out_shape=(
            jax.ShapeDtypeStruct((NZERO * ROWS, COLS), bf16),
            jax.ShapeDtypeStruct((ROWS, COLS), f32),
            jax.ShapeDtypeStruct((WQ // 128, 128), f32),
            jax.ShapeDtypeStruct((1, WK), f32),
            jax.ShapeDtypeStruct((1, WK), f32),
            jax.ShapeDtypeStruct((norm_rows, 128), f32),
        ),
        in_specs=[hbm] * 8,
        out_specs=(pl.BlockSpec(memory_space=pltpu.VMEM),) * 6,
        scratch_shapes=[
            pltpu.VMEM((ROWS, COLS), f32),
            pltpu.VMEM((ROWS, COLS), f32),
            pltpu.VMEM((NZERO, 1, COLS), f32),
            pltpu.VMEM((NORM,), f32),
            pltpu.VMEM((NORM,), f32),
            pltpu.VMEM((NZERO, NW, 1, 128), f32),
            dma((4, 6)),
            dma((2,)),
            dma((NZERO,)), dma((NZERO,)),
            dma((NW,)), dma((NW,)),
            dma((NZERO,)), dma((NZERO,)),
            dma((4, len(ORDER))), dma((4, len(ORDER))),
        ],
        compiler_params=pltpu.CompilerParams(
            collective_id=0, has_side_effects=True, vmem_limit_bytes=26 * 2**20
        ),
    )(*(pltpu.with_memory_space_constraint(v, pltpu.HBM) for v in (tq, sq, tk, sk, tv, sv, nt, ns)))
    whole = NZERO * ROWS
    outs = pl.pallas_call(
        write_kernel,
        name="write",
        out_shape=(
            jax.ShapeDtypeStruct((whole, WQ), bf16),
            jax.ShapeDtypeStruct((whole, WK), bf16),
            jax.ShapeDtypeStruct((whole, WK), bf16),
            jax.ShapeDtypeStruct((WQ // 128, 128), f32),
            jax.ShapeDtypeStruct((1, WK), f32),
            jax.ShapeDtypeStruct((1, WK), f32),
            jax.ShapeDtypeStruct((norm_rows, 128), bf16),
            jax.ShapeDtypeStruct((ROWS, WQ), f32),
            jax.ShapeDtypeStruct((ROWS, WK), f32),
            jax.ShapeDtypeStruct((ROWS, WK), f32),
        ),
        in_specs=[anyspace] * 5 + [pl.BlockSpec(memory_space=pltpu.VMEM)],
        out_specs=(hbm,) * 10,
        scratch_shapes=[pltpu.VMEM((norm_rows, 128), bf16), dma((10,))],
        compiler_params=pltpu.CompilerParams(vmem_limit_bytes=2 * 2**20),
    )(*gathered)
    rq, rk, rv, cq, ck, cv, norm, lq, lk, lv = outs
    return (
        rq, rk, rv, cq.reshape(-1), ck.reshape(-1), cv.reshape(-1), norm.reshape(-1), lq, lk, lv
    )


def solution(mesh):
    both = P("zero", "width")
    in_specs = (both,) * 6 + (P(("zero", "width")),) * 2
    out_specs = (
        (P(None, "width"),) * 3 + (P("width"),) * 3 + (P(),) + (both,) * 3
    )
    return jax.shard_map(body, mesh=mesh, in_specs=in_specs, out_specs=out_specs, check_vma=False)
```

time: 158 us -> 106 us (0.67)
  Pallas kernels: 0 us -> 105 us
  blocking collectives: 82 us -> 0 us
  waiting for transfers between devices: 42.3 us -> 0 us
  local copies, waits for them, and re-layouts: 15.2 us -> 0 us
  between operations: 14.3 us -> 0.65 us
  other arithmetic: 3.64 us -> 0 us
    pallas_call x0 -> x2, Pallas kernels: none -> 105 us  [the longest x1 98.8 us: body(): pl.pallas_call(gather_kernel, name='gather', out_shape=(jax.ShapeDtypeStr...]
    unnamed x1 -> x0, blocking collectives: 66.3 us -> none
    all_gather x1 -> x0, waiting for transfers between devices: 42.3 us -> none  [sent_together(): whole = lax.all_gather(both, axis, axis=dim, tiled=True)]
    all_to_all x1 -> x0, blocking collectives: 15.6 us -> none  [sent_to_all(): lax.all_to_all(jnp.broadcast_to(array[None], (size, *array.shape)), axis,...]
    split x2 -> x0, local copies, waits for them, and re-layouts: 14.8 us -> none  [sent_together(): jnp.split(whole, [sum(widths[:k]) for k in range(1, len(widths))], axis=a...]
    reduce_sum x3 -> x0, other arithmetic: 2.41 us -> none  [the longest x1 2.27 us: body(): jnp.sum(latest_query * latest_query, axis=0)]
  transfers between devices with their start and end apart: 1 -> 0, of which waited for: 1 -> 0; matrix products, arithmetic and copies ran while one was open for 0% -> 0% of each run, Pallas kernels for 0% -> 0%
where the time goes in v1:
time: 106 us
  Pallas kernels  105 us (99%)
    pallas_call x1, Pallas kernels, body(): pl.pallas_call(gather_kernel, name='gather', out_shape=(jax.ShapeDtypeStr...  98.8 us
    pallas_call x1, Pallas kernels, body(): pl.pallas_call(write_kernel, name='write', out_shape=(jax.ShapeDtypeStruc...  6.67 us

profile of v1, /device:TPU:0, one launch (start us, length us, event | category | flops | bytes accessed | tf_op | source)
XLA Modules:
  0.0 106.1 jit_solution(5010479064642283784)
XLA Ops:
  0.6 98.8 %gather.1 = (bf16[7168,1152]{1,0:T(8,128)(2,1)S(1)}, f32[448,1152]{1,0:T(8,128)S(1)}, f32[7,128]{1,0:T(8,128)S(1)}, f32[1,128]{1,0:T(1,128)S(1)}, f32[1,128]{1,0:T(1,128)S(1)}, /*index=5*/f32[56,128]{1,0:T(8,128)S(1)}) custom-call(f32[448,896]{1,0:T(8,128)} %tq.1, f32[448,896]{1,0:T(8,128)} %sq.1, f32[448,128]{1,0:T(8,128)} %tk.1, f32[448,128]{1,0:T(8,128)} %sk.1, ...), custom_call_target="tpu_custom_call" | custom-call | tf_op jit(solution)/shard_map/gather/pallas_call | solution.py:259
  99.4 6.7 %write.1 = (bf16[7168,896]{1,0:T(8,128)(2,1)}, bf16[7168,128]{1,0:T(8,128)(2,1)}, bf16[7168,128]{1,0:T(8,128)(2,1)}, f32[7,128]{1,0:T(8,128)}, f32[1,128]{1,0:T(...) custom-call(bf16[7168,1152]{1,0:T(8,128)(2,1)S(1)} %get-tuple-elemen, ...), custom_call_target="tpu_custom_call" | custom-call | tf_op jit(solution)/shard_map/write/pallas_call | solution.py:291

commit v2 on v1

--- a/solution.py
+++ b/solution.py
@@ -17,6 +17,7 @@
 COLS = WQ + 2 * WK
 QUARTER = ROWS // 4
 SLAB = 16
+EARLY = 16
 NORM = 56
 
 ORDER = (
@@ -44,16 +45,13 @@
 def gather_kernel(
     tq, sq, tk, sk, tv, sv, nt, ns,
     all_ref, lat_ref, cq_ref, ck_ref, cv_ref, norm_ref,
-    tbuf, sbuf, sums, ntb, nsb, nbuf,
+    tbuf, sbuf, sums, ntb, nsb, nbuf, early,
     load_sem, nload_sem, sum_send, sum_recv, na_send, na_recv, nb_send, nb_recv,
-    send_sem, recv_sem,
+    send_sem, recv_sem, early_send, early_recv,
 ):
     me = lax.axis_index("zero")
     wide = lax.axis_index("width")
     z, y = me // NY, me % NY
-
-    def at(zz, yy):
-        return lax.rem(zz + 2 * NZ, NZ) * NY + lax.rem(yy + 2 * NY, NY)
 
     barrier = pltpu.get_barrier_semaphore()
     for d in range(1, NZERO):
@@ -126,6 +124,26 @@
         )
         copy.start()
         across.append(copy)
+
+    def at(zz, yy):
+        return lax.rem(zz + 2 * NZ, NZ) * NY + lax.rem(yy + 2 * NY, NY)
+
+    def beside(link, steps):
+        ring, sign = LINKS[link]
+        return at(z + sign * steps, y) if ring == "z" else at(z, y + sign * steps)
+
+    ahead = {}
+    for which in range(2):
+        for link in range(4):
+            p = PARTNER[link] if which else link
+            copy = pltpu.make_async_remote_copy(
+                src_ref=lat_ref.at[pl.ds(p * QUARTER, EARLY)], dst_ref=early.at[link, which],
+                send_sem=early_send.at[link, which], recv_sem=early_recv.at[link, which],
+                device_id=(beside(link, 1), wide), device_id_type=MESH,
+            )
+            copy.start()
+            ahead[link, which] = copy
+
     for copy in small:
         copy.wait()
 
@@ -141,9 +159,9 @@
 
     copies = {}
 
-    def piece(p, zz, yy):
-        first = at(zz, yy) * ROWS + p * QUARTER
-        return pl.ds(pl.multiple_of(first, QUARTER), QUARTER)
+    def piece(p, zz, yy, skip):
+        first = at(zz, yy) * ROWS + p * QUARTER + skip
+        return pl.ds(pl.multiple_of(first, SLAB), QUARTER - skip)
 
     def start(link, slot):
         ring, sign = LINKS[link]
@@ -160,27 +178,39 @@
             elif j == 3:
                 copies[p, SLOT["one", 2]].wait_recv()
             steps = {ring: k, LINKS[p][0]: j}
-        rows = piece(p, z - sign * steps.get("z", 0), y - sign * steps.get("y", 0))
-        target = at(z + sign, y) if ring == "z" else at(z, y + sign)
+        skip = 0 if any(steps.values()) else EARLY
+        rows = piece(p, z - sign * steps.get("z", 0), y - sign * steps.get("y", 0), skip)
         copy = pltpu.make_async_remote_copy(
             src_ref=all_ref.at[rows], dst_ref=all_ref.at[rows],
             send_sem=send_sem.at[link, slot], recv_sem=recv_sem.at[link, slot],
-            device_id=(target, wide), device_id_type=MESH,
+            device_id=(beside(link, 1), wide), device_id_type=MESH,
         )
         copy.start()
         copies[link, slot] = copy
 
+    def narrow(src, first, there, steps):
+        def step(i, _):
+            rows = pl.ds(pl.multiple_of(first + i * SLAB, SLAB), SLAB)
+            out = pl.ds(pl.multiple_of(there + i * SLAB, SLAB), SLAB)
+            all_ref[out, :] = (src[rows, :] * inverse).astype(jnp.bfloat16)
+            return 0
+
+        lax.fori_loop(0, steps, step, 0)
+
     for p in range(4):
-        def narrow(i, _):
-            rows = pl.ds(pl.multiple_of(p * QUARTER + i * SLAB, SLAB), SLAB)
-            there = pl.ds(pl.multiple_of(me * ROWS + p * QUARTER + i * SLAB, SLAB), SLAB)
-            all_ref[there, :] = (lat_ref[rows, :] * inverse).astype(jnp.bfloat16)
-            return 0
-
-        lax.fori_loop(0, QUARTER // SLAB, narrow, 0)
+        first = p * QUARTER + EARLY
+        narrow(lat_ref, first, me * ROWS + first, (QUARTER - EARLY) // SLAB)
         start(p, 0)
     for link in range(4):
         start(link, 1)
+    for p in range(4):
+        first = p * QUARTER
+        narrow(lat_ref, first, me * ROWS + first, EARLY // SLAB)
+    for link in range(4):
+        for which in range(2):
+            ahead[link, which].wait()
+            p = PARTNER[link] if which else link
+            narrow(early.at[link, which], 0, beside(link, -1) * ROWS + p * QUARTER, EARLY // SLAB)
 
     for copy in across:
         copy.wait()
@@ -276,12 +306,14 @@
             pltpu.VMEM((NORM,), f32),
             pltpu.VMEM((NORM,), f32),
             pltpu.VMEM((NZERO, NW, 1, 128), f32),
+            pltpu.VMEM((4, 2, EARLY, COLS), f32),
             dma((4, 6)),
             dma((2,)),
             dma((NZERO,)), dma((NZERO,)),
             dma((NW,)), dma((NW,)),
             dma((NZERO,)), dma((NZERO,)),
             dma((4, len(ORDER))), dma((4, len(ORDER))),
+            dma((4, 2)), dma((4, 2)),
         ],
         compiler_params=pltpu.CompilerParams(
             collective_id=0, has_side_effects=True, vmem_limit_bytes=26 * 2**20

time: 106 us -> 105 us (level)
    pallas_call x1, Pallas kernels: 98.8 us -> 97.3 us  [body(): pl.pallas_call(gather_kernel, name='gather', out_shape=(jax.ShapeDtypeStr...]
where the time goes in v2:
time: 105 us
  Pallas kernels  104 us (99%)
    pallas_call x1, Pallas kernels, body(): pl.pallas_call(gather_kernel, name='gather', out_shape=(jax.ShapeDtypeStr...  97.3 us
    pallas_call x1, Pallas kernels, body(): pl.pallas_call(write_kernel, name='write', out_shape=(jax.ShapeDtypeStruc...  6.67 us

profile of v2, /device:TPU:0, one launch (start us, length us, event | category | flops | bytes accessed | tf_op | source)
XLA Modules:
  0.0 104.6 jit_solution(14044680370147677626)
XLA Ops:
  0.6 97.3 %gather.1 = (bf16[7168,1152]{1,0:T(8,128)(2,1)S(1)}, f32[448,1152]{1,0:T(8,128)S(1)}, f32[7,128]{1,0:T(8,128)S(1)}, f32[1,128]{1,0:T(1,128)S(1)}, f32[1,128]{1,0:T(1,128)S(1)}, /*index=5*/f32[56,128]{1,0:T(8,128)S(1)}) custom-call(f32[448,896]{1,0:T(8,128)} %tq.1, f32[448,896]{1,0:T(8,128)} %sq.1, f32[448,128]{1,0:T(8,128)} %tk.1, f32[448,128]{1,0:T(8,128)} %sk.1, ...), custom_call_target="tpu_custom_call" | custom-call | tf_op jit(solution)/shard_map/gather/pallas_call | solution.py:289
  98.0 6.7 %write.1 = (bf16[7168,896]{1,0:T(8,128)(2,1)}, bf16[7168,128]{1,0:T(8,128)(2,1)}, bf16[7168,128]{1,0:T(8,128)(2,1)}, f32[7,128]{1,0:T(8,128)}, f32[1,128]{1,0:T(...) custom-call(bf16[7168,1152]{1,0:T(8,128)(2,1)S(1)} %get-tuple-elemen, ...), custom_call_target="tpu_custom_call" | custom-call | tf_op jit(solution)/shard_map/write/pallas_call | solution.py:323

commit v3 on v2

--- a/solution.py
+++ b/solution.py
@@ -47,7 +47,7 @@
     all_ref, lat_ref, cq_ref, ck_ref, cv_ref, norm_ref,
     tbuf, sbuf, sums, ntb, nsb, nbuf, early,
     load_sem, nload_sem, sum_send, sum_recv, na_send, na_recv, nb_send, nb_recv,
-    send_sem, recv_sem, early_send, early_recv,
+    send_sem, recv_sem, early_send, early_recv, group_sem, go_sem,
 ):
     me = lax.axis_index("zero")
     wide = lax.axis_index("width")
@@ -58,10 +58,13 @@
         pl.semaphore_signal(
             barrier, inc=1, device_id=(lax.rem(me + d, NZERO), wide), device_id_type=MESH
         )
-    for d in range(1, NW):
-        pl.semaphore_signal(
-            barrier, inc=1, device_id=(me, lax.rem(wide + d, NW)), device_id_type=MESH
-        )
+
+    @pl.when(me == 0)
+    def _():
+        for d in range(1, NW):
+            pl.semaphore_signal(
+                barrier, inc=1, device_id=(me, lax.rem(wide + d, NW)), device_id_type=MESH
+            )
 
     loads = []
     for c in range(4):
@@ -99,12 +102,14 @@
 
         acc = lax.fori_loop(0, QUARTER // SLAB, average, acc)
     sums[me] = jnp.sum(acc, axis=0, keepdims=True)
-    for copy in nload:
-        copy.wait()
-    mine = (ntb[...] + nsb[...]).reshape(1, NORM)
-    nbuf[me, wide] = jnp.concatenate([mine, jnp.zeros((1, 128 - NORM), jnp.float32)], axis=1)
-
-    pl.semaphore_wait(barrier, NZERO - 1 + NW - 1)
+
+    @pl.when(me == 0)
+    def _():
+        pl.semaphore_wait(barrier, NZERO - 1 + NW - 1)
+
+    @pl.when(me != 0)
+    def _():
+        pl.semaphore_wait(barrier, NZERO - 1)
 
     small = []
     for d in range(1, NZERO):
@@ -115,16 +120,6 @@
         )
         copy.start()
         small.append(copy)
-    across = []
-    for d in range(1, NW):
-        copy = pltpu.make_async_remote_copy(
-            src_ref=nbuf.at[me, wide], dst_ref=nbuf.at[me, wide],
-            send_sem=na_send.at[d], recv_sem=na_recv.at[d],
-            device_id=(me, lax.rem(wide + d, NW)), device_id_type=MESH,
-        )
-        copy.start()
-        across.append(copy)
-
     def at(zz, yy):
         return lax.rem(zz + 2 * NZ, NZ) * NY + lax.rem(yy + 2 * NY, NY)
 
@@ -143,6 +138,18 @@
             )
             copy.start()
             ahead[link, which] = copy
+
+    @pl.when(me == 0)
+    def _():
+        for d in range(1, NW):
+            pl.semaphore_signal(
+                group_sem, inc=1, device_id=(me, lax.rem(wide + d, NW)), device_id_type=MESH
+            )
+
+    for copy in nload:
+        copy.wait()
+    mine = (ntb[...] + nsb[...]).reshape(1, NORM)
+    nbuf[me, wide] = jnp.concatenate([mine, jnp.zeros((1, 128 - NORM), jnp.float32)], axis=1)
 
     for copy in small:
         copy.wait()
@@ -212,6 +219,34 @@
             p = PARTNER[link] if which else link
             narrow(early.at[link, which], 0, beside(link, -1) * ROWS + p * QUARTER, EARLY // SLAB)
 
+    for slot in range(2, 4):
+        for link in range(4):
+            start(link, slot)
+
+    @pl.when(me == 0)
+    def _():
+        pl.semaphore_wait(group_sem, NW - 1)
+        for d in range(1, NZERO):
+            pl.semaphore_signal(go_sem, inc=1, device_id=(d, wide), device_id_type=MESH)
+
+    @pl.when(me != 0)
+    def _():
+        pl.semaphore_wait(go_sem, 1)
+
+    across = []
+    for d in range(1, NW):
+        copy = pltpu.make_async_remote_copy(
+            src_ref=nbuf.at[me, wide], dst_ref=nbuf.at[me, wide],
+            send_sem=na_send.at[d], recv_sem=na_recv.at[d],
+            device_id=(me, lax.rem(wide + d, NW)), device_id_type=MESH,
+        )
+        copy.start()
+        across.append(copy)
+
+    for slot in range(4, 6):
+        for link in range(4):
+            start(link, slot)
+
     for copy in across:
         copy.wait()
     on = []
@@ -224,7 +259,7 @@
         copy.start()
         on.append(copy)
 
-    for slot in range(2, 6):
+    for slot in range(6, 8):
         for link in range(4):
             start(link, slot)
 
@@ -239,7 +274,7 @@
             row = jnp.where((lane >= shift) & (lane < shift + NORM), moved, row)
         norm_ref[pl.ds(r, 1), :] = row
 
-    for slot in range(6, len(ORDER)):
+    for slot in range(8, len(ORDER)):
         for link in range(4):
             start(link, slot)
 
@@ -314,6 +349,7 @@
             dma((NZERO,)), dma((NZERO,)),
             dma((4, len(ORDER))), dma((4, len(ORDER))),
             dma((4, 2)), dma((4, 2)),
+            pltpu.SemaphoreType.REGULAR, pltpu.SemaphoreType.REGULAR,
         ],
         compiler_params=pltpu.CompilerParams(
             collective_id=0, has_side_effects=True, vmem_limit_bytes=26 * 2**20

time: 105 us -> 104 us (level)
  no operation moved by 1% of the time
where the time goes in v3:
time: 104 us
  Pallas kernels  104 us (100%)
    pallas_call x1, Pallas kernels, body(): pl.pallas_call(gather_kernel, name='gather', out_shape=(jax.ShapeDtypeStr...  96.9 us
    pallas_call x1, Pallas kernels, body(): pl.pallas_call(write_kernel, name='write', out_shape=(jax.ShapeDtypeStruc...  6.67 us

profile of v3, /device:TPU:0, one launch (start us, length us, event | category | flops | bytes accessed | tf_op | source)
XLA Modules:
  0.0 104.2 jit_solution(16265030158679681914)
XLA Ops:
  0.6 96.9 %gather.1 = (bf16[7168,1152]{1,0:T(8,128)(2,1)S(1)}, f32[448,1152]{1,0:T(8,128)S(1)}, f32[7,128]{1,0:T(8,128)S(1)}, f32[1,128]{1,0:T(1,128)S(1)}, f32[1,128]{1,0:T(1,128)S(1)}, /*index=5*/f32[56,128]{1,0:T(8,128)S(1)}) custom-call(f32[448,896]{1,0:T(8,128)} %tq.1, f32[448,896]{1,0:T(8,128)} %sq.1, f32[448,128]{1,0:T(8,128)} %tk.1, f32[448,128]{1,0:T(8,128)} %sk.1, ...), custom_call_target="tpu_custom_call" | custom-call | tf_op jit(solution)/shard_map/gather/pallas_call | solution.py:324
  97.6 6.7 %write.1 = (bf16[7168,896]{1,0:T(8,128)(2,1)}, bf16[7168,128]{1,0:T(8,128)(2,1)}, bf16[7168,128]{1,0:T(8,128)(2,1)}, f32[7,128]{1,0:T(8,128)}, f32[1,128]{1,0:T(...) custom-call(bf16[7168,1152]{1,0:T(8,128)(2,1)S(1)} %get-tuple-elemen, ...), custom_call_target="tpu_custom_call" | custom-call | tf_op jit(solution)/shard_map/write/pallas_call | solution.py:359

commit v4 on v3

--- a/solution.py
+++ b/solution.py
@@ -37,7 +37,21 @@
     ("two", 2, 2),
     ("two", 3, 2),
 )
-SLOT = {entry: at for at, entry in enumerate(ORDER)}
+GROUPS = (
+    (2, (("one", 0),)),
+    (4, (("one", 1),)),
+    (6, (("two", 0, 0), ("one", 2))),
+    (8, (("two", 1, 0), ("two", 2, 0))),
+    (10, (("two", 0, 1), ("two", 3, 0))),
+    (12, (("two", 1, 1), ("two", 2, 1))),
+    (14, (("two", 3, 1),)),
+)
+GROUP = {entry: g for g, (_, entries) in enumerate(GROUPS) for entry in entries}
+FIRST = (("one", 0), ("two", 0, 0))
+OTHERS = sorted(
+    ((dz, dy) for dz in range(NZ) for dy in range(NY) if dz or dy),
+    key=lambda d: -min(d[0], NZ - d[0]) - min(d[1], NY - d[1]),
+)
 LINKS = (("y", 1), ("y", -1), ("z", 1), ("z", -1))
 PARTNER = (2, 3, 0, 1)
 
@@ -45,18 +59,24 @@
 def gather_kernel(
     tq, sq, tk, sk, tv, sv, nt, ns,
     all_ref, lat_ref, cq_ref, ck_ref, cv_ref, norm_ref,
-    tbuf, sbuf, sums, ntb, nsb, nbuf, early,
+    inbuf, sums, ntb, nsb, nbuf, early,
     load_sem, nload_sem, sum_send, sum_recv, na_send, na_recv, nb_send, nb_recv,
-    send_sem, recv_sem, early_send, early_recv, group_sem, go_sem,
+    send_sem, recv_sem, last_sem, early_send, early_recv, group_sem, go_sem,
 ):
     me = lax.axis_index("zero")
     wide = lax.axis_index("width")
     z, y = me // NY, me % NY
 
+    def at(zz, yy):
+        return lax.rem(zz + 2 * NZ, NZ) * NY + lax.rem(yy + 2 * NY, NY)
+
+    def drain(ref, sem):
+        pltpu.make_async_copy(ref, ref, sem).wait()
+
     barrier = pltpu.get_barrier_semaphore()
-    for d in range(1, NZERO):
+    for dz, dy in OTHERS:
         pl.semaphore_signal(
-            barrier, inc=1, device_id=(lax.rem(me + d, NZERO), wide), device_id_type=MESH
+            barrier, inc=1, device_id=(at(z + dz, y + dy), wide), device_id_type=MESH
         )
 
     @pl.when(me == 0)
@@ -66,21 +86,14 @@
                 barrier, inc=1, device_id=(me, lax.rem(wide + d, NW)), device_id_type=MESH
             )
 
-    loads = []
     for c in range(4):
         rows = pl.ds(c * QUARTER, QUARTER)
-        group = []
-        for i, (src, buf, first, width) in enumerate((
-            (tq, tbuf, 0, WQ), (sq, sbuf, 0, WQ),
-            (tk, tbuf, WQ, WK), (sk, sbuf, WQ, WK),
-            (tv, tbuf, WQ + WK, WK), (sv, sbuf, WQ + WK, WK),
+        for i, (src, first, width) in enumerate((
+            (tq, 0, WQ), (sq, 0, WQ), (tk, WQ, WK), (sk, WQ, WK), (tv, WQ + WK, WK), (sv, WQ + WK, WK)
         )):
-            copy = pltpu.make_async_copy(
-                src.at[rows], buf.at[rows, pl.ds(first, width)], load_sem.at[c, i]
-            )
-            copy.start()
-            group.append(copy)
-        loads.append(group)
+            pltpu.make_async_copy(
+                src.at[rows], inbuf.at[i % 2, rows, pl.ds(first, width)], load_sem.at[c]
+            ).start()
     nload = (
         pltpu.make_async_copy(nt, ntb, nload_sem.at[0]),
         pltpu.make_async_copy(ns, nsb, nload_sem.at[1]),
@@ -90,12 +103,11 @@
 
     acc = jnp.zeros((8, COLS), jnp.float32)
     for c in range(4):
-        for copy in loads[c]:
-            copy.wait()
+        drain(inbuf.at[:, pl.ds(c * QUARTER, QUARTER)], load_sem.at[c])
 
         def average(i, acc):
             rows = pl.ds(pl.multiple_of(c * QUARTER + i * SLAB, SLAB), SLAB)
-            latest = keep_rate * sbuf[rows, :] + (1.0 - keep_rate) * tbuf[rows, :]
+            latest = keep_rate * inbuf[1, rows, :] + (1.0 - keep_rate) * inbuf[0, rows, :]
             lat_ref[rows, :] = latest
             square = latest * latest
             return acc + square[:8] + square[8:]
@@ -111,33 +123,24 @@
     def _():
         pl.semaphore_wait(barrier, NZERO - 1)
 
-    small = []
-    for d in range(1, NZERO):
-        copy = pltpu.make_async_remote_copy(
-            src_ref=sums.at[me], dst_ref=sums.at[me],
-            send_sem=sum_send.at[d], recv_sem=sum_recv.at[d],
-            device_id=(lax.rem(me + d, NZERO), wide), device_id_type=MESH,
-        )
-        copy.start()
-        small.append(copy)
-    def at(zz, yy):
-        return lax.rem(zz + 2 * NZ, NZ) * NY + lax.rem(yy + 2 * NY, NY)
+    for dz, dy in OTHERS:
+        pltpu.make_async_remote_copy(
+            src_ref=sums.at[me], dst_ref=sums.at[me], send_sem=sum_send, recv_sem=sum_recv,
+            device_id=(at(z + dz, y + dy), wide), device_id_type=MESH,
+        ).start()
 
     def beside(link, steps):
         ring, sign = LINKS[link]
         return at(z + sign * steps, y) if ring == "z" else at(z, y + sign * steps)
 
-    ahead = {}
     for which in range(2):
         for link in range(4):
             p = PARTNER[link] if which else link
-            copy = pltpu.make_async_remote_copy(
+            pltpu.make_async_remote_copy(
                 src_ref=lat_ref.at[pl.ds(p * QUARTER, EARLY)], dst_ref=early.at[link, which],
-                send_sem=early_send.at[link, which], recv_sem=early_recv.at[link, which],
+                send_sem=early_send, recv_sem=early_recv,
                 device_id=(beside(link, 1), wide), device_id_type=MESH,
-            )
-            copy.start()
-            ahead[link, which] = copy
+            ).start()
 
     @pl.when(me == 0)
     def _():
@@ -151,8 +154,9 @@
     mine = (ntb[...] + nsb[...]).reshape(1, NORM)
     nbuf[me, wide] = jnp.concatenate([mine, jnp.zeros((1, 128 - NORM), jnp.float32)], axis=1)
 
-    for copy in small:
-        copy.wait()
+    some = sums.at[pl.ds(0, NZERO - 1)]
+    drain(some, sum_send)
+    drain(some, sum_recv)
 
     total = sums[0]
     for d in range(1, NZERO):
@@ -164,36 +168,31 @@
     cv_ref[...] = scale[:, WQ + WK :]
     inverse = jnp.broadcast_to(1.0 / scale, (SLAB, COLS))
 
-    copies = {}
-
     def piece(p, zz, yy, skip):
         first = at(zz, yy) * ROWS + p * QUARTER + skip
         return pl.ds(pl.multiple_of(first, SLAB), QUARTER - skip)
 
+    def count(entry):
+        return QUARTER - EARLY if entry in FIRST else QUARTER
+
     def start(link, slot):
         ring, sign = LINKS[link]
         entry = ORDER[slot]
+        for g, (when, entries) in enumerate(GROUPS):
+            if when == slot:
+                drain(all_ref.at[pl.ds(0, sum(map(count, entries)))], recv_sem.at[link, g])
         if entry[0] == "one":
-            p, j, k = link, 0, entry[1]
-            if k > 0:
-                copies[link, SLOT["one", k - 1]].wait_recv()
-            steps = {ring: k}
+            p, steps = link, {ring: entry[1]}
         else:
-            p, j, k = PARTNER[link], entry[1], entry[2]
-            if k > 0:
-                copies[link, SLOT["two", j, k - 1]].wait_recv()
-            elif j == 3:
-                copies[p, SLOT["one", 2]].wait_recv()
-            steps = {ring: k, LINKS[p][0]: j}
-        skip = 0 if any(steps.values()) else EARLY
+            p = PARTNER[link]
+            steps = {ring: entry[2], LINKS[p][0]: entry[1]}
+        skip = QUARTER - count(entry)
         rows = piece(p, z - sign * steps.get("z", 0), y - sign * steps.get("y", 0), skip)
-        copy = pltpu.make_async_remote_copy(
-            src_ref=all_ref.at[rows], dst_ref=all_ref.at[rows],
-            send_sem=send_sem.at[link, slot], recv_sem=recv_sem.at[link, slot],
+        arrived = recv_sem.at[link, GROUP[entry]] if entry in GROUP else last_sem
+        pltpu.make_async_remote_copy(
+            src_ref=all_ref.at[rows], dst_ref=all_ref.at[rows], send_sem=send_sem, recv_sem=arrived,
             device_id=(beside(link, 1), wide), device_id_type=MESH,
-        )
-        copy.start()
-        copies[link, slot] = copy
+        ).start()
 
     def narrow(src, first, there, steps):
         def step(i, _):
@@ -213,9 +212,10 @@
     for p in range(4):
         first = p * QUARTER
         narrow(lat_ref, first, me * ROWS + first, EARLY // SLAB)
+    drain(early, early_send)
+    drain(early, early_recv)
     for link in range(4):
         for which in range(2):
-            ahead[link, which].wait()
             p = PARTNER[link] if which else link
             narrow(early.at[link, which], 0, beside(link, -1) * ROWS + p * QUARTER, EARLY // SLAB)
 
@@ -233,38 +233,32 @@
     def _():
         pl.semaphore_wait(go_sem, 1)
 
-    across = []
     for d in range(1, NW):
-        copy = pltpu.make_async_remote_copy(
-            src_ref=nbuf.at[me, wide], dst_ref=nbuf.at[me, wide],
-            send_sem=na_send.at[d], recv_sem=na_recv.at[d],
+        pltpu.make_async_remote_copy(
+            src_ref=nbuf.at[me, wide], dst_ref=nbuf.at[me, wide], send_sem=na_send, recv_sem=na_recv,
             device_id=(me, lax.rem(wide + d, NW)), device_id_type=MESH,
-        )
-        copy.start()
-        across.append(copy)
+        ).start()
 
     for slot in range(4, 6):
         for link in range(4):
             start(link, slot)
 
-    for copy in across:
-        copy.wait()
-    on = []
-    for d in range(1, NZERO):
-        copy = pltpu.make_async_remote_copy(
-            src_ref=nbuf.at[me], dst_ref=nbuf.at[me],
-            send_sem=nb_send.at[d], recv_sem=nb_recv.at[d],
-            device_id=(lax.rem(me + d, NZERO), wide), device_id_type=MESH,
-        )
-        copy.start()
-        on.append(copy)
+    row = nbuf.at[me, pl.ds(0, NW - 1)]
+    drain(row, na_send)
+    drain(row, na_recv)
+    for dz, dy in OTHERS:
+        pltpu.make_async_remote_copy(
+            src_ref=nbuf.at[me], dst_ref=nbuf.at[me], send_sem=nb_send, recv_sem=nb_recv,
+            device_id=(at(z + dz, y + dy), wide), device_id_type=MESH,
+        ).start()
 
     for slot in range(6, 8):
         for link in range(4):
             start(link, slot)
 
-    for copy in on:
-        copy.wait()
+    some = nbuf.at[pl.ds(0, NZERO - 1)]
+    drain(some, nb_send)
+    drain(some, nb_recv)
     lane = lax.broadcasted_iota(jnp.int32, (1, 128), 1)
     for r in range(NZERO * NW * NORM // 128):
         row = jnp.zeros((1, 128), jnp.float32)
@@ -278,15 +272,8 @@
         for link in range(4):
             start(link, slot)
 
-    for slot in range(len(ORDER)):
-        for link in range(4):
-            copies[link, slot].wait_send()
-    waited = {("one", 0), ("one", 1), ("one", 2)}
-    waited |= {("two", j, k) for j in range(4) for k in range(2)}
-    for entry in ORDER:
-        if entry not in waited:
-            for link in range(4):
-                copies[link, SLOT[entry]].wait_recv()
+    drain(all_ref.at[pl.ds(0, 4 * sum(map(count, ORDER)))], send_sem)
+    drain(all_ref.at[pl.ds(0, 4 * QUARTER * (len(ORDER) - len(GROUP)))], last_sem)
 
 
 def write_kernel(
@@ -335,20 +322,19 @@
         in_specs=[hbm] * 8,
         out_specs=(pl.BlockSpec(memory_space=pltpu.VMEM),) * 6,
         scratch_shapes=[
-            pltpu.VMEM((ROWS, COLS), f32),
-            pltpu.VMEM((ROWS, COLS), f32),
+            pltpu.VMEM((2, ROWS, COLS), f32),
             pltpu.VMEM((NZERO, 1, COLS), f32),
             pltpu.VMEM((NORM,), f32),
             pltpu.VMEM((NORM,), f32),
             pltpu.VMEM((NZERO, NW, 1, 128), f32),
             pltpu.VMEM((4, 2, EARLY, COLS), f32),
-            dma((4, 6)),
+            dma((4,)),
             dma((2,)),
-            dma((NZERO,)), dma((NZERO,)),
-            dma((NW,)), dma((NW,)),
-            dma((NZERO,)), dma((NZERO,)),
-            dma((4, len(ORDER))), dma((4, len(ORDER))),
-            dma((4, 2)), dma((4, 2)),
+            dma, dma,
+            dma, dma,
+            dma, dma,
+            dma, dma((4, len(GROUPS))), dma,
+            dma, dma,
             pltpu.SemaphoreType.REGULAR, pltpu.SemaphoreType.REGULAR,
         ],
         compiler_params=pltpu.CompilerParams(

time: 104 us -> 102 us (0.981)
  Pallas kernels: 104 us -> 102 us
    pallas_call x1, Pallas kernels: 96.9 us -> 95 us  [body(): pl.pallas_call(gather_kernel, name='gather', out_shape=(jax.ShapeDtypeStr...]
where the time goes in v4:
time: 102 us
  Pallas kernels  102 us (100%)
    pallas_call x1, Pallas kernels, body(): pl.pallas_call(gather_kernel, name='gather', out_shape=(jax.ShapeDtypeStr...  95 us
    pallas_call x1, Pallas kernels, body(): pl.pallas_call(write_kernel, name='write', out_shape=(jax.ShapeDtypeStruc...  6.67 us

profile of v4, /device:TPU:0, one launch (start us, length us, event | category | flops | bytes accessed | tf_op | source)
XLA Modules:
  0.0 102.3 jit_solution(11924217440940510695)
XLA Ops:
  0.6 95.0 %gather.1 = (bf16[7168,1152]{1,0:T(8,128)(2,1)S(1)}, f32[448,1152]{1,0:T(8,128)S(1)}, f32[7,128]{1,0:T(8,128)S(1)}, f32[1,128]{1,0:T(1,128)S(1)}, f32[1,128]{1,0:T(1,128)S(1)}, /*index=5*/f32[56,128]{1,0:T(8,128)S(1)}) custom-call(f32[448,896]{1,0:T(8,128)} %tq.1, f32[448,896]{1,0:T(8,128)} %sq.1, f32[448,128]{1,0:T(8,128)} %tk.1, f32[448,128]{1,0:T(8,128)} %sk.1, ...), custom_call_target="tpu_custom_call" | custom-call | tf_op jit(solution)/shard_map/gather/pallas_call | solution.py:311
  95.7 6.7 %write.1 = (bf16[7168,896]{1,0:T(8,128)(2,1)}, bf16[7168,128]{1,0:T(8,128)(2,1)}, bf16[7168,128]{1,0:T(8,128)(2,1)}, f32[7,128]{1,0:T(8,128)}, f32[1,128]{1,0:T(...) custom-call(bf16[7168,1152]{1,0:T(8,128)(2,1)S(1)} %get-tuple-elemen, ...), custom_call_target="tpu_custom_call" | custom-call | tf_op jit(solution)/shard_map/write/pallas_call | solution.py:345

commit v5 on v4

--- a/solution.py
+++ b/solution.py
@@ -60,7 +60,7 @@
     tq, sq, tk, sk, tv, sv, nt, ns,
     all_ref, lat_ref, cq_ref, ck_ref, cv_ref, norm_ref,
     inbuf, sums, ntb, nsb, nbuf, early,
-    load_sem, nload_sem, sum_send, sum_recv, na_send, na_recv, nb_send, nb_recv,
+    load_sem, nload_sem, sum_send, sum_recv, na_send, na_recv,
     send_sem, recv_sem, last_sem, early_send, early_recv, group_sem, go_sem,
 ):
     me = lax.axis_index("zero")
@@ -113,7 +113,12 @@
             return acc + square[:8] + square[8:]
 
         acc = lax.fori_loop(0, QUARTER // SLAB, average, acc)
-    sums[me] = jnp.sum(acc, axis=0, keepdims=True)
+    for copy in nload:
+        copy.wait()
+    gain = (ntb[...] + nsb[...]).reshape(1, NORM)
+    sums[me] = jnp.concatenate(
+        [jnp.sum(acc, axis=0, keepdims=True), gain, jnp.zeros((1, 128 - NORM), jnp.float32)], axis=1
+    )
 
     @pl.when(me == 0)
     def _():
@@ -149,18 +154,13 @@
                 group_sem, inc=1, device_id=(me, lax.rem(wide + d, NW)), device_id_type=MESH
             )
 
-    for copy in nload:
-        copy.wait()
-    mine = (ntb[...] + nsb[...]).reshape(1, NORM)
-    nbuf[me, wide] = jnp.concatenate([mine, jnp.zeros((1, 128 - NORM), jnp.float32)], axis=1)
-
     some = sums.at[pl.ds(0, NZERO - 1)]
     drain(some, sum_send)
     drain(some, sum_recv)
 
-    total = sums[0]
+    total = sums[0, :, :COLS]
     for d in range(1, NZERO):
-        total = total + sums[d]
+        total = total + sums[d, :, :COLS]
     scale = jnp.sqrt(total)
     for r in range(WQ // 128):
         cq_ref[pl.ds(r, 1), :] = scale[:, r * 128 : (r + 1) * 128]
@@ -170,7 +170,7 @@
 
     def piece(p, zz, yy, skip):
         first = at(zz, yy) * ROWS + p * QUARTER + skip
-        return pl.ds(pl.multiple_of(first, SLAB), QUARTER - skip)
+        return pl.ds(pl.multiple_of(first, 8), QUARTER - skip)
 
     def count(entry):
         return QUARTER - EARLY if entry in FIRST else QUARTER
@@ -178,9 +178,6 @@
     def start(link, slot):
         ring, sign = LINKS[link]
         entry = ORDER[slot]
-        for g, (when, entries) in enumerate(GROUPS):
-            if when == slot:
-                drain(all_ref.at[pl.ds(0, sum(map(count, entries)))], recv_sem.at[link, g])
         if entry[0] == "one":
             p, steps = link, {ring: entry[1]}
         else:
@@ -188,40 +185,51 @@
             steps = {ring: entry[2], LINKS[p][0]: entry[1]}
         skip = QUARTER - count(entry)
         rows = piece(p, z - sign * steps.get("z", 0), y - sign * steps.get("y", 0), skip)
-        arrived = recv_sem.at[link, GROUP[entry]] if entry in GROUP else last_sem
+        arrived = recv_sem.at[GROUP[entry]] if entry in GROUP else last_sem
         pltpu.make_async_remote_copy(
             src_ref=all_ref.at[rows], dst_ref=all_ref.at[rows], send_sem=send_sem, recv_sem=arrived,
             device_id=(beside(link, 1), wide), device_id_type=MESH,
         ).start()
 
-    def narrow(src, first, there, steps):
+    def starts(first, last):
+        for slot in range(first, last):
+            for g, (when, entries) in enumerate(GROUPS):
+                if when == slot:
+                    drain(all_ref.at[pl.ds(0, 4 * sum(map(count, entries)))], recv_sem.at[g])
+            for link in range(4):
+                start(link, slot)
+
+    def narrow(src, first, there, count):
+        def some(at_row, height):
+            rows = pl.ds(pl.multiple_of(first + at_row, 8), height)
+            out = pl.ds(pl.multiple_of(there + at_row, 8), height)
+            all_ref[out, :] = (src[rows, :] * inverse[:height]).astype(jnp.bfloat16)
+
         def step(i, _):
-            rows = pl.ds(pl.multiple_of(first + i * SLAB, SLAB), SLAB)
-            out = pl.ds(pl.multiple_of(there + i * SLAB, SLAB), SLAB)
-            all_ref[out, :] = (src[rows, :] * inverse).astype(jnp.bfloat16)
+            some(i * SLAB, SLAB)
             return 0
 
-        lax.fori_loop(0, steps, step, 0)
+        lax.fori_loop(0, count // SLAB, step, 0)
+        if count % SLAB:
+            some(count // SLAB * SLAB, count % SLAB)
 
     for p in range(4):
         first = p * QUARTER + EARLY
-        narrow(lat_ref, first, me * ROWS + first, (QUARTER - EARLY) // SLAB)
+        narrow(lat_ref, first, me * ROWS + first, QUARTER - EARLY)
         start(p, 0)
     for link in range(4):
         start(link, 1)
     for p in range(4):
         first = p * QUARTER
-        narrow(lat_ref, first, me * ROWS + first, EARLY // SLAB)
+        narrow(lat_ref, first, me * ROWS + first, EARLY)
     drain(early, early_send)
     drain(early, early_recv)
     for link in range(4):
         for which in range(2):
             p = PARTNER[link] if which else link
-            narrow(early.at[link, which], 0, beside(link, -1) * ROWS + p * QUARTER, EARLY // SLAB)
-
-    for slot in range(2, 4):
-        for link in range(4):
-            start(link, slot)
+            narrow(early.at[link, which], 0, beside(link, -1) * ROWS + p * QUARTER, EARLY)
+
+    starts(2, 4)
 
     @pl.when(me == 0)
     def _():
@@ -233,44 +241,30 @@
     def _():
         pl.semaphore_wait(go_sem, 1)
 
+    nbuf[wide] = sums[:, :, COLS:]
     for d in range(1, NW):
         pltpu.make_async_remote_copy(
-            src_ref=nbuf.at[me, wide], dst_ref=nbuf.at[me, wide], send_sem=na_send, recv_sem=na_recv,
+            src_ref=nbuf.at[wide], dst_ref=nbuf.at[wide], send_sem=na_send, recv_sem=na_recv,
             device_id=(me, lax.rem(wide + d, NW)), device_id_type=MESH,
         ).start()
 
-    for slot in range(4, 6):
-        for link in range(4):
-            start(link, slot)
-
-    row = nbuf.at[me, pl.ds(0, NW - 1)]
-    drain(row, na_send)
-    drain(row, na_recv)
-    for dz, dy in OTHERS:
-        pltpu.make_async_remote_copy(
-            src_ref=nbuf.at[me], dst_ref=nbuf.at[me], send_sem=nb_send, recv_sem=nb_recv,
-            device_id=(at(z + dz, y + dy), wide), device_id_type=MESH,
-        ).start()
-
-    for slot in range(6, 8):
-        for link in range(4):
-            start(link, slot)
-
-    some = nbuf.at[pl.ds(0, NZERO - 1)]
-    drain(some, nb_send)
-    drain(some, nb_recv)
+    starts(4, 6)
+
+    starts(6, 8)
+
+    some = nbuf.at[pl.ds(0, NW - 1)]
+    drain(some, na_send)
+    drain(some, na_recv)
     lane = lax.broadcasted_iota(jnp.int32, (1, 128), 1)
     for r in range(NZERO * NW * NORM // 128):
         row = jnp.zeros((1, 128), jnp.float32)
         for d in range(128 * r // NORM, (128 * r + 127) // NORM + 1):
             shift = d * NORM - 128 * r
-            moved = pltpu.roll(nbuf[d // NW, d % NW], shift % 128, 1)
+            moved = pltpu.roll(nbuf[d % NW, d // NW], shift % 128, 1)
             row = jnp.where((lane >= shift) & (lane < shift + NORM), moved, row)
         norm_ref[pl.ds(r, 1), :] = row
 
-    for slot in range(8, len(ORDER)):
-        for link in range(4):
-            start(link, slot)
+    starts(8, len(ORDER))
 
     drain(all_ref.at[pl.ds(0, 4 * sum(map(count, ORDER)))], send_sem)
     drain(all_ref.at[pl.ds(0, 4 * QUARTER * (len(ORDER) - len(GROUP)))], last_sem)
@@ -323,17 +317,16 @@
         out_specs=(pl.BlockSpec(memory_space=pltpu.VMEM),) * 6,
         scratch_shapes=[
             pltpu.VMEM((2, ROWS, COLS), f32),
-            pltpu.VMEM((NZERO, 1, COLS), f32),
+            pltpu.VMEM((NZERO, 1, COLS + 128), f32),
             pltpu.VMEM((NORM,), f32),
             pltpu.VMEM((NORM,), f32),
-            pltpu.VMEM((NZERO, NW, 1, 128), f32),
+            pltpu.VMEM((NW, NZERO, 1, 128), f32),
             pltpu.VMEM((4, 2, EARLY, COLS), f32),
             dma((4,)),
             dma((2,)),
             dma, dma,
             dma, dma,
-            dma, dma,
-            dma, dma((4, len(GROUPS))), dma,
+            dma, dma((len(GROUPS),)), dma,
             dma, dma,
             pltpu.SemaphoreType.REGULAR, pltpu.SemaphoreType.REGULAR,
         ],

time: 102 us -> 102 us (level)
  no operation moved by 1% of the time
where the time goes in v5:
time: 102 us; the launch traced here: 101 us
  Pallas kernels  101 us (99%)
    pallas_call x1, Pallas kernels, body(): pl.pallas_call(gather_kernel, name='gather', out_shape=(jax.ShapeDtypeStr...  94.1 us
    pallas_call x1, Pallas kernels, body(): pl.pallas_call(write_kernel, name='write', out_shape=(jax.ShapeDtypeStruc...  6.67 us

profile of v5, /device:TPU:0, one launch (start us, length us, event | category | flops | bytes accessed | tf_op | source)
XLA Modules:
  0.0 101.4 jit_solution(1217744066729636378)
XLA Ops:
  0.6 94.1 %gather.1 = (bf16[7168,1152]{1,0:T(8,128)(2,1)S(1)}, f32[448,1152]{1,0:T(8,128)S(1)}, f32[7,128]{1,0:T(8,128)S(1)}, f32[1,128]{1,0:T(1,128)S(1)}, f32[1,128]{1,0:T(1,128)S(1)}, /*index=5*/f32[56,128]{1,0:T(8,128)S(1)}) custom-call(f32[448,896]{1,0:T(8,128)} %tq.1, f32[448,896]{1,0:T(8,128)} %sq.1, f32[448,128]{1,0:T(8,128)} %tk.1, f32[448,128]{1,0:T(8,128)} %sk.1, ...), custom_call_target="tpu_custom_call" | custom-call | tf_op jit(solution)/shard_map/gather/pallas_call | solution.py:305
  94.8 6.7 %write.1 = (bf16[7168,896]{1,0:T(8,128)(2,1)}, bf16[7168,128]{1,0:T(8,128)(2,1)}, bf16[7168,128]{1,0:T(8,128)(2,1)}, f32[7,128]{1,0:T(8,128)}, f32[1,128]{1,0:T(...) custom-call(bf16[7168,1152]{1,0:T(8,128)(2,1)S(1)} %get-tuple-elemen, ...), custom_call_target="tpu_custom_call" | custom-call | tf_op jit(solution)/shard_map/write/pallas_call | solution.py:338

commit v6 on v5

--- a/solution.py
+++ b/solution.py
@@ -86,8 +86,8 @@
                 barrier, inc=1, device_id=(me, lax.rem(wide + d, NW)), device_id_type=MESH
             )
 
-    for c in range(4):
-        rows = pl.ds(c * QUARTER, QUARTER)
+    for c in range(2):
+        rows = pl.ds(c * 2 * QUARTER, 2 * QUARTER)
         for i, (src, first, width) in enumerate((
             (tq, 0, WQ), (sq, 0, WQ), (tk, WQ, WK), (sk, WQ, WK), (tv, WQ + WK, WK), (sv, WQ + WK, WK)
         )):
@@ -102,17 +102,17 @@
         copy.start()
 
     acc = jnp.zeros((8, COLS), jnp.float32)
-    for c in range(4):
-        drain(inbuf.at[:, pl.ds(c * QUARTER, QUARTER)], load_sem.at[c])
+    for c in range(2):
+        drain(inbuf.at[:, pl.ds(c * 2 * QUARTER, 2 * QUARTER)], load_sem.at[c])
 
         def average(i, acc):
-            rows = pl.ds(pl.multiple_of(c * QUARTER + i * SLAB, SLAB), SLAB)
+            rows = pl.ds(pl.multiple_of(c * 2 * QUARTER + i * SLAB, SLAB), SLAB)
             latest = keep_rate * inbuf[1, rows, :] + (1.0 - keep_rate) * inbuf[0, rows, :]
             lat_ref[rows, :] = latest
             square = latest * latest
             return acc + square[:8] + square[8:]
 
-        acc = lax.fori_loop(0, QUARTER // SLAB, average, acc)
+        acc = lax.fori_loop(0, 2 * QUARTER // SLAB, average, acc, unroll=7)
     for copy in nload:
         copy.wait()
     gain = (ntb[...] + nsb[...]).reshape(1, NORM)
@@ -162,10 +162,6 @@
     for d in range(1, NZERO):
         total = total + sums[d, :, :COLS]
     scale = jnp.sqrt(total)
-    for r in range(WQ // 128):
-        cq_ref[pl.ds(r, 1), :] = scale[:, r * 128 : (r + 1) * 128]
-    ck_ref[...] = scale[:, WQ : WQ + WK]
-    cv_ref[...] = scale[:, WQ + WK :]
     inverse = jnp.broadcast_to(1.0 / scale, (SLAB, COLS))
 
     def piece(p, zz, yy, skip):
@@ -209,7 +205,7 @@
             some(i * SLAB, SLAB)
             return 0
 
-        lax.fori_loop(0, count // SLAB, step, 0)
+        lax.fori_loop(0, count // SLAB, step, 0, unroll=True)
         if count % SLAB:
             some(count // SLAB * SLAB, count % SLAB)
 
@@ -219,6 +215,10 @@
         start(p, 0)
     for link in range(4):
         start(link, 1)
+    for r in range(WQ // 128):
+        cq_ref[pl.ds(r, 1), :] = scale[:, r * 128 : (r + 1) * 128]
+    ck_ref[...] = scale[:, WQ : WQ + WK]
+    cv_ref[...] = scale[:, WQ + WK :]
     for p in range(4):
         first = p * QUARTER
         narrow(lat_ref, first, me * ROWS + first, EARLY)

time: 102 us -> 101 us (level)
  no operation moved by 1% of the time
where the time goes in v6:
time: 101 us
  Pallas kernels  101 us (100%)
    pallas_call x1, Pallas kernels, body(): pl.pallas_call(gather_kernel, name='gather', out_shape=(jax.ShapeDtypeStr...  94 us
    pallas_call x1, Pallas kernels, body(): pl.pallas_call(write_kernel, name='write', out_shape=(jax.ShapeDtypeStruc...  6.67 us

profile of v6, /device:TPU:0, one launch (start us, length us, event | category | flops | bytes accessed | tf_op | source)
XLA Modules:
  0.0 101.3 jit_solution(13539350380684266429)
XLA Ops:
  0.6 94.0 %gather.1 = (bf16[7168,1152]{1,0:T(8,128)(2,1)S(1)}, f32[448,1152]{1,0:T(8,128)S(1)}, f32[7,128]{1,0:T(8,128)S(1)}, f32[1,128]{1,0:T(1,128)S(1)}, f32[1,128]{1,0:T(1,128)S(1)}, /*index=5*/f32[56,128]{1,0:T(8,128)S(1)}) custom-call(f32[448,896]{1,0:T(8,128)} %tq.1, f32[448,896]{1,0:T(8,128)} %sq.1, f32[448,128]{1,0:T(8,128)} %tk.1, f32[448,128]{1,0:T(8,128)} %sk.1, ...), custom_call_target="tpu_custom_call" | custom-call | tf_op jit(solution)/shard_map/gather/pallas_call | solution.py:305
  94.6 6.7 %write.1 = (bf16[7168,896]{1,0:T(8,128)(2,1)}, bf16[7168,128]{1,0:T(8,128)(2,1)}, bf16[7168,128]{1,0:T(8,128)(2,1)}, f32[7,128]{1,0:T(8,128)}, f32[1,128]{1,0:T(...) custom-call(bf16[7168,1152]{1,0:T(8,128)(2,1)S(1)} %get-tuple-elemen, ...), custom_call_target="tpu_custom_call" | custom-call | tf_op jit(solution)/shard_map/write/pallas_call | solution.py:338

commit v7 on v6

--- a/solution.py
+++ b/solution.py
@@ -213,7 +213,9 @@
         first = p * QUARTER + EARLY
         narrow(lat_ref, first, me * ROWS + first, QUARTER - EARLY)
         start(p, 0)
-    for link in range(4):
+        if p >= 2:
+            start(p, 1)
+    for link in range(2):
         start(link, 1)
     for r in range(WQ // 128):
         cq_ref[pl.ds(r, 1), :] = scale[:, r * 128 : (r + 1) * 128]

time: 101 us -> 101 us (level)
  no operation moved by 1% of the time
where the time goes in v7:
time: 101 us
  Pallas kernels  101 us (100%)
    pallas_call x1, Pallas kernels, body(): pl.pallas_call(gather_kernel, name='gather', out_shape=(jax.ShapeDtypeStr...  94 us
    pallas_call x1, Pallas kernels, body(): pl.pallas_call(write_kernel, name='write', out_shape=(jax.ShapeDtypeStruc...  6.67 us

profile of v7, /device:TPU:0, one launch (start us, length us, event | category | flops | bytes accessed | tf_op | source)
XLA Modules:
  0.0 101.3 jit_solution(3987306296665832530)
XLA Ops:
  0.6 94.0 %gather.1 = (bf16[7168,1152]{1,0:T(8,128)(2,1)S(1)}, f32[448,1152]{1,0:T(8,128)S(1)}, f32[7,128]{1,0:T(8,128)S(1)}, f32[1,128]{1,0:T(1,128)S(1)}, f32[1,128]{1,0:T(1,128)S(1)}, /*index=5*/f32[56,128]{1,0:T(8,128)S(1)}) custom-call(f32[448,896]{1,0:T(8,128)} %tq.1, f32[448,896]{1,0:T(8,128)} %sq.1, f32[448,128]{1,0:T(8,128)} %tk.1, f32[448,128]{1,0:T(8,128)} %sk.1, ...), custom_call_target="tpu_custom_call" | custom-call | tf_op jit(solution)/shard_map/gather/pallas_call | solution.py:307
  94.6 6.7 %write.1 = (bf16[7168,896]{1,0:T(8,128)(2,1)}, bf16[7168,128]{1,0:T(8,128)(2,1)}, bf16[7168,128]{1,0:T(8,128)(2,1)}, f32[7,128]{1,0:T(8,128)}, f32[1,128]{1,0:T(...) custom-call(bf16[7168,1152]{1,0:T(8,128)(2,1)S(1)} %get-tuple-elemen, ...), custom_call_target="tpu_custom_call" | custom-call | tf_op jit(solution)/shard_map/write/pallas_call | solution.py:340
